TPU v7x, 32 devices: a whole 2x2x4 slice. The times are simulated.
32 devices in a mesh: epoch: 8 (over z, y), blend: 4 (over x, core).
Axes of the slice: x: 2, y: 2, z: 4, core: 2. Of those that a mesh axis runs over, the one named last changes fastest.
Arguments:
- models: float32 [4, 16, 6, 4096], P('blend', 'epoch'), may hold values from -6 to 6
- observed: bfloat16 [8, 64, 4096], P('epoch', 'blend'), may hold values from -6 to 6
- weights: float32 [8, 64], P('epoch', 'blend'), may hold values from 0.5 to 2
- coverage: int32 [8, 64], P('epoch', 'blend'), may hold values from 0 to 1, as said below
- offsets: int32 [8, 64, 2], P('epoch', 'blend'), may hold values from 0 to 63
- counts: int32 [4, 16], P('blend', 'epoch'), may hold values from 1 to 8, as said below
- psf_y: bfloat16 [8, 4096], P('epoch'), may hold values from -0.75 to 0.75
- resample_y: bfloat16 [8, 4096], P('epoch'), may hold values from -0.75 to 0.75
- psf_x: bfloat16 [8, 4096], P('epoch'), may hold values from -0.75 to 0.75
- resample_x: bfloat16 [8, 4096], P('epoch'), may hold values from -0.75 to 0.75
Outputs:
- updated: float32 [4, 16, 6, 4096], P('blend', 'epoch')
Inputs may be any that keep to these rules, and one draw needn't show every extreme that they name: `coverage`: every blend is seen by one epoch or more. counts of blend b is the sum of coverage over all epochs for b.
All inputs are finite; a program needn't handle non-finite values.
Results may differ from a plain program's by a relative error of at most 0.0017.
Values may be sent and summed in bfloat16 or wider, within the bound.
A program may use at most 128 MiB of HBM per device.

v0:
```python
import jax
import jax.numpy as jnp
from jax import lax
from jax.sharding import PartitionSpec as P

CUT = 64
BANDS = 6
PIX2 = 4096
step_size = 0.5


def roll_forward(image, down, across):
    side = image.shape[0]
    doubled = jnp.concatenate([image, image], axis=0)
    rows = lax.dynamic_slice_in_dim(doubled, down, side, 0)
    doubled = jnp.concatenate([rows, rows], axis=1)
    return lax.dynamic_slice_in_dim(doubled, across, side, 1)


def one_epoch(model_low, observed, scale, offsets, left, right, band):
    side = left.shape[0]
    count = observed.shape[0]
    chosen = lax.dynamic_index_in_dim(model_low, band, 1, keepdims=False)
    shifted = jax.vmap(roll_forward)(chosen, offsets[:, 0], offsets[:, 1])
    blurred = jnp.einsum("ij,bjk->bik", left, shifted, preferred_element_type=jnp.float32).astype(
        jnp.bfloat16
    )
    predicted = jnp.einsum("bik,lk->bil", blurred, right, preferred_element_type=jnp.float32)
    target = observed.reshape(count, side, side).astype(jnp.float32)
    misfit = (scale[:, None, None] * (predicted - target)).astype(jnp.bfloat16)
    back = jnp.einsum("ji,bjk->bik", left, misfit, preferred_element_type=jnp.float32).astype(
        jnp.bfloat16
    )
    term = jnp.einsum("bik,kl->bil", back, right, preferred_element_type=jnp.float32)
    return jax.vmap(roll_forward)(term, side - offsets[:, 0], side - offsets[:, 1])


def on_device(
    models, observed, weights, coverage, offsets, counts, psf_y, resample_y, psf_x, resample_x
):
    ep_dev = observed.shape[0]
    group_size = lax.axis_size("epoch")
    all_epochs = ep_dev * group_size
    anchor = lax.axis_index("epoch") * ep_dev
    lefts = jnp.einsum(
        "eij,ejk->eik",
        psf_y.reshape(ep_dev, CUT, CUT),
        resample_y.reshape(ep_dev, CUT, CUT),
        preferred_element_type=jnp.float32,
    ).astype(jnp.bfloat16)
    rights = jnp.einsum(
        "eij,ejk->eik",
        psf_x.reshape(ep_dev, CUT, CUT),
        resample_x.reshape(ep_dev, CUT, CUT),
        preferred_element_type=jnp.float32,
    ).astype(jnp.bfloat16)
    scale = weights * coverage.astype(jnp.float32)
    epoch_bands = (anchor + 0) * BANDS // all_epochs
    first_band = anchor * BANDS // all_epochs
    model_low = models.astype(jnp.bfloat16)
    piece = lax.all_gather(model_low, "epoch", axis=1, tiled=True)
    count = piece.shape[1]
    blocks = piece[0].reshape(count, BANDS, CUT, CUT)
    terms = one_epoch(
        blocks, observed[0], scale[0], offsets[0], lefts[0], rights[0], epoch_bands
    ).reshape(count, PIX2)
    total = jnp.zeros((count, 2, PIX2), jnp.float32)
    slot = epoch_bands - first_band
    current = lax.dynamic_index_in_dim(total, slot, 1, keepdims=False)
    total = lax.dynamic_update_index_in_dim(total, current + terms, slot, 1)
    received = lax.all_to_all(total, "epoch", split_axis=0, concat_axis=1, tiled=True)
    slot_count = received.shape[1]
    position = jnp.arange(slot_count, dtype=jnp.int32)
    source = position // 2
    band_of = source * ep_dev * BANDS // all_epochs + position % 2
    selector = (band_of[:, None] == jnp.arange(BANDS, dtype=jnp.int32)[None, :]).astype(jnp.float32)
    gradient = jnp.einsum("bkp,kc->bcp", received, selector, precision=lax.Precision.HIGHEST)
    divisor = counts[0].astype(jnp.float32)[:, None, None]
    updated = models[0] - step_size * gradient / divisor
    return updated[None]


def solution(mesh):
    return jax.shard_map(
        on_device,
        mesh=mesh,
        in_specs=(
            P("blend", "epoch", None, None),
            P("epoch", "blend", None),
            P("epoch", "blend"),
            P("epoch", "blend"),
            P("epoch", "blend", None),
            P("blend", "epoch"),
            P("epoch", None),
            P("epoch", None),
            P("epoch", None),
            P("epoch", None),
        ),
        out_specs=P("blend", "epoch", None, None),
        check_vma=False,
    )
```

profile of v0, /device:TPU:0, one launch (start us, length us, event | category | flops | bytes accessed | tf_op | source)
XLA Modules:
  0.0 66.9 jit_solution(17146201242047359278)
XLA Ops:
  0.0 1.0 %convert_element_type.47 = bf16[1,2,6,4096]{3,1,2,0:T(2,128)(2,1)S(1)} convert(f32[1,2,6,4096]{3,1,2,0:T(2,128)} %param.10) | non-fusion elementwise | flops 49152 | bytes 294912 | tf_op jit(solution)/shard_map/convert_element_type | solution.py:60
  1.0 0.1 copy.60
  1.1 34.6 %all_gather.3 = bf16[1,16,6,4096]{3,2,0,1:T(8,128)(2,1)S(1)} all-gather(bf16[1,2,6,4096]{3,2,0,1:T(8,128)(2,1)S(1)} %copy.60), channel_id=1, replica_groups=mesh['epoch'=8,'blend'=4] {'epoch'}, dimensions={1}, use_global_device_ids=true | all-gather | bytes 884736 | tf_op jit(solution)/shard_map/all_gather | solution.py:61
  35.7 0.4 copy.61
  36.1 0.0 copy-start.6
  36.1 1.7 %reshape_squeeze.4 = bf16[16,6,64,64]{3,2,0,1:T(8,128)(2,1)S(1)} reshape(bf16[1,16,6,4096]{3,1,2,0:T(8,128)(2,1)S(1)} %copy.61) | data formatting | bytes 1572864 | tf_op jit(solution)/shard_map/reshape;squeeze | solution.py:63
  37.9 0.2 copy.86
  38.1 0.1 pad_maximum_fusion
  38.2 0.0 copy-done.6
  38.2 0.0 copy-start.2
  38.2 0.0 copy-start.3
  38.2 0.0 copy-start.4
  38.2 0.0 copy-start.5
  38.3 0.0 copy-start.1
  38.3 1.4 %gather_fusion = bf16[16,64,64]{2,0,1:T(8,128)(2,1)S(1)} fusion(bf16[16,128,64]{2,0,1:T(8,128)(2,1)S(1)} %pad_maximum_fusion, s32[16]{0:T(128)S(1)} %get-tuple-element.6), kind=kCustom, calls=%fused_computation | custom fusion | bytes 262336 | tf_op jit(solution)/shard_map/vmap()/gather | solution.py:15
  39.6 0.1 pad_maximum_fusion.3
  39.8 0.5 copy.63
  40.4 0.1 reduce.2
  40.4 0.1 reshape.76
  40.5 0.1 reduce.3
  40.5 0.1 reshape.77
  40.6 0.1 reduce
  40.7 0.1 reshape.74
  40.8 0.1 reduce.1
  40.8 0.0 copy-start.7
  40.8 0.0 copy-start.8
  40.9 0.1 reshape.75
  40.9 0.2 reshape.78
  41.2 1.4 %gather_fusion.1 = bf16[16,64,64]{1,0,2:T(8,128)(2,1)S(1)} fusion(bf16[16,64,128]{1,0,2:T(8,128)(2,1)S(1)} %copy.63, s32[16]{0:T(128)S(1)} %get-tuple-element.7), kind=kCustom, calls=%fused_computation.1 | custom fusion | bytes 262336 | tf_op jit(solution)/shard_map/vmap()/gather | solution.py:17
  42.5 0.1 fusion.10
  42.7 0.1 fusion.9
  42.8 0.4 fusion.5
  43.3 0.4 fusion.8
  43.7 0.2 pad_maximum_fusion.1
  43.9 0.5 copy.69
  44.4 1.3 %gather_fusion.2 = f32[16,64,64]{2,0,1:T(8,128)S(1)} fusion(f32[16,128,64]{2,0,1:T(8,128)S(1)} %copy.69, s32[16]{0:T(128)S(1)} %get-tuple-element.8), kind=kCustom, calls=%fused_computation.2 | custom fusion | bytes 524480 | tf_op jit(solution)/shard_map/vmap()/gather | solution.py:15
  45.8 0.2 pad_maximum_fusion.2
  46.0 0.6 copy.70
  46.6 1.3 %gather_fusion.3 = f32[16,64,64]{1,0,2:T(8,128)S(1)} fusion(f32[16,64,128]{1,0,2:T(8,128)S(1)} %copy.70, s32[16]{0:T(128)S(1)} %get-tuple-element.5), kind=kCustom, calls=%fused_computation.3 | custom fusion | bytes 524480 | tf_op jit(solution)/shard_map/vmap()/gather | solution.py:17
  47.9 0.3 copy.71
  48.2 0.0 copy-start.9
  48.2 0.3 broadcast_in_dim.8
  48.5 1.0 %dynamic_update_slice.4.clone = f32[16,2,4096]{2,1,0:T(2,128)} pad(f32[16,1,4096]{2,1,0:T(1,128)S(1)} %broadcast_in_dim.8, f32[]{:T(128)} %constant.85.clone.1), padding=0_0x0_1x0_0 | pad | bytes 786436 | tf_op jit(solution)/shard_map/jit(dynamic_update_index_in_dim)/dynamic_update_slice | solution.py:70
  49.5 5.5 %all-to-all-start = ((f32[16,2,4096]{2,1,0:T(2,128)}), f32[16,2,4096]{2,1,0:T(2,128)S(1)}, u32[]{:S(2)}, u32[]{:S(2)}) async-start(f32[16,2,4096]{2,1,0:T(2,128)} %dynamic_update_slice.4.clone), calls=%async_computation | async-start | bytes 1048576 | tf_op jit(solution)/shard_map/all_to_all | solution.py:71
  55.0 10.3 %all-to-all-done = f32[16,2,4096]{2,1,0:T(2,128)S(1)} async-done(((f32[16,2,4096]{2,1,0:T(2,128)}), f32[16,2,4096]{2,1,0:T(2,128)S(1)}, u32[]{:S(2)}, u32[]{:S(2)}) %all-to-all-start) | async-done | bytes 524320 | tf_op jit(solution)/shard_map/all_to_all | solution.py:71
  65.3 0.4 all_to_all.16
  65.7 0.4 fusion.3
  66.1 0.8 %copy.74 = f32[1,2,6,4096]{3,1,2,0:T(2,128)} copy(f32[1,2,6,4096]{3,2,1,0:T(8,128)S(1)} %fusion.3) | data formatting | bytes 393216 | tf_op jit(solution)/shard_map/broadcast_in_dim | solution.py:80
  (16 shorter events, 0.1 us)
Async XLA Ops:
  36.1 2.1 %copy-start.6 = (s32[1,16,2]{1,2,0:T(2,128)S(1)}, s32[1,16,2]{1,2,0:T(2,128)}, u32[]{:S(2)}) copy-start(s32[1,16,2]{1,2,0:T(2,128)} %param.14) | copy-start | bytes 388
  38.2 2.1 %copy-start.2 = (bf16[1,4096]{1,0:T(2,128)(2,1)S(1)}, bf16[1,4096]{1,0:T(2,128)(2,1)}, u32[]{:S(2)}) copy-start(bf16[1,4096]{1,0:T(2,128)(2,1)} %param.18) | copy-start | bytes 24580
  38.2 2.3 %copy-start.3 = (bf16[1,4096]{1,0:T(2,128)(2,1)S(1)}, bf16[1,4096]{1,0:T(2,128)(2,1)}, u32[]{:S(2)}) copy-start(bf16[1,4096]{1,0:T(2,128)(2,1)} %param.19) | copy-start | bytes 24580
  38.2 2.4 %copy-start.4 = (bf16[1,4096]{1,0:T(2,128)(2,1)S(1)}, bf16[1,4096]{1,0:T(2,128)(2,1)}, u32[]{:S(2)}) copy-start(bf16[1,4096]{1,0:T(2,128)(2,1)} %param.16) | copy-start | bytes 24580
  38.2 2.5 %copy-start.5 = (bf16[1,4096]{1,0:T(2,128)(2,1)S(1)}, bf16[1,4096]{1,0:T(2,128)(2,1)}, u32[]{:S(2)}) copy-start(bf16[1,4096]{1,0:T(2,128)(2,1)} %param.17) | copy-start | bytes 24580
  38.3 2.7 %copy-start.1 = (bf16[1,16,4096]{2,1,0:T(8,128)(2,1)S(1)}, bf16[1,16,4096]{2,1,0:T(8,128)(2,1)}, u32[]{:S(2)}) copy-start(bf16[1,16,4096]{2,1,0:T(8,128)(2,1)} %param.11) | copy-start | bytes 393220
  40.8 2.0 %copy-start.7 = (f32[1,16]{1,0:T(1,128)S(1)}, f32[1,16]{1,0:T(1,128)}, u32[]{:S(2)}) copy-start(f32[1,16]{1,0:T(1,128)} %param.12) | copy-start | bytes 196
  40.8 1.9 %copy-start.8 = (s32[1,16]{1,0:T(1,128)S(1)}, s32[1,16]{1,0:T(1,128)}, u32[]{:S(2)}) copy-start(s32[1,16]{1,0:T(1,128)} %param.13) | copy-start | bytes 196
  48.2 6.9 %copy-start.9 = (s32[1,2]{1,0:T(1,128)S(1)}, s32[1,2]{1,0:T(1,128)}, u32[]{:S(2)}) copy-start(s32[1,2]{1,0:T(1,128)} %param.15) | copy-start | bytes 28
  49.5 16.2 %copy-start = (f32[1,2,6,4096]{3,1,2,0:T(2,128)S(1)}, f32[1,2,6,4096]{3,1,2,0:T(2,128)}, u32[]{:S(2)}) copy-start(f32[1,2,6,4096]{3,1,2,0:T(2,128)} %param.10) | copy-start | bytes 589828
  49.5 15.8 %all-to-all-start = ((f32[16,2,4096]{2,1,0:T(2,128)}), f32[16,2,4096]{2,1,0:T(2,128)S(1)}, u32[]{:S(2)}, u32[]{:S(2)}) async-start(f32[16,2,4096]{2,1,0:T(2,128)} %dynamic_update_slice.4.clone), calls=%async_computation | async-start | bytes 1048576 | tf_op jit(solution)/shard_map/all_to_all | solution.py:71
where the time goes:
time: 67.1 us; the launch traced here: 66.9 us
  blocking collectives  34.6 us (52%)
  local copies, waits for them, and re-layouts  12.8 us (19%)
  waiting for transfers between devices  10.3 us (15%)
  starting transfers between devices  5.52 us (8%)
  other arithmetic  1.9 us (3%)
  matrix products  1.48 us (2%)
    all_gather x1, blocking collectives, on_device(): piece = lax.all_gather(model_low, 'epoch', axis=1, tiled=True)  34.6 us
    all_to_all x1, waiting for transfers between devices, on_device(): lax.all_to_all(total, 'epoch', split_axis=0, concat_axis=1, tiled=True)  10.3 us
    all_to_all x1, starting transfers between devices, on_device(): lax.all_to_all(total, 'epoch', split_axis=0, concat_axis=1, tiled=True)  5.52 us
    gather x3, local copies, waits for them, and re-layouts, roll_forward(): return lax.dynamic_slice_in_dim(doubled, across, side, 1)  2.97 us
    gather x2, local copies, waits for them, and re-layouts, roll_forward(): rows = lax.dynamic_slice_in_dim(doubled, down, side, 0)  2.71 us
    another operation x1, local copies, waits for them, and re-layouts, on_device(): blocks = piece[0].reshape(count, BANDS, CUT, CUT)  1.72 us
  transfers between devices with their start and end apart: 1, of which 1 were waited for; matrix products, arithmetic and copies ran while one was open for 0% of the time, Pallas kernels for 0%

commit v1 on v0

--- a/solution.py
+++ b/solution.py
@@ -58,7 +58,8 @@
     epoch_bands = (anchor + 0) * BANDS // all_epochs
     first_band = anchor * BANDS // all_epochs
     model_low = models.astype(jnp.bfloat16)
-    piece = lax.all_gather(model_low, "epoch", axis=1, tiled=True)
+    block_last = jnp.stack(jax.lax.axis_size("epoch") * [model_low], axis=0)
+    piece = jnp.concatenate(jax.lax.all_to_all(block_last, "epoch", 0, 0), axis=1)
     count = piece.shape[1]
     blocks = piece[0].reshape(count, BANDS, CUT, CUT)
     terms = one_epoch(

time: 67.1 us -> 62.9 us (0.937)
  blocking collectives: 34.6 us -> 0 us
  waiting for transfers between devices: 10.3 us -> 32.9 us
  starting transfers between devices: 5.52 us -> 11 us
  local copies, waits for them, and re-layouts: 12.8 us -> 14.9 us
    all_gather x1 -> x0, blocking collectives: 34.6 us -> none  [on_device(): piece = lax.all_gather(model_low, 'epoch', axis=1, tiled=True)]
    all_to_all x0 -> x1, waiting for transfers between devices: none -> 18.3 us  [on_device(): jax.lax.all_to_all(block_last, 'epoch', 0, 0)]
    all_to_all x0 -> x1, starting transfers between devices: none -> 7.33 us  [on_device(): jax.lax.all_to_all(block_last, 'epoch', 0, 0)]
    all_to_all x1, waiting for transfers between devices: 10.3 us -> 14.6 us  [on_device(): lax.all_to_all(total, 'epoch', split_axis=0, concat_axis=1, tiled=True)]
    all_to_all x1, starting transfers between devices: 5.52 us -> 3.7 us  [on_device(): lax.all_to_all(total, 'epoch', split_axis=0, concat_axis=1, tiled=True)]
    another operation x3 -> x5, local copies, waits for them, and re-layouts: 0.25 us -> 1.98 us  [the longest x1 1.65 us: on_device(): block_last = jnp.stack(jax.lax.axis_size('epoch') * [model_low], axis=0)]
    convert_element_type x1, local copies, waits for them, and re-layouts: 0.21 us -> 1.02 us  [one_epoch(): target = observed.reshape(count, side, side).astype(jnp.float32)]
    all_to_all x0 -> x1, local copies, waits for them, and re-layouts: none -> 0.78 us  [on_device(): jax.lax.all_to_all(block_last, 'epoch', 0, 0)]
  transfers between devices with their start and end apart: 1 -> 2, of which waited for: 1 -> 2; matrix products, arithmetic and copies ran while one was open for 0% -> 3% of each run, Pallas kernels for 0% -> 0%
where the time goes in v1:
time: 62.9 us; the launch traced here: 62.6 us
  waiting for transfers between devices  32.9 us (52%)
  local copies, waits for them, and re-layouts  14.9 us (24%)
  starting transfers between devices  11 us (17%)
  other arithmetic  1.96 us (3%)
  matrix products  1.48 us (2%)
    all_to_all x1, waiting for transfers between devices, on_device(): jax.lax.all_to_all(block_last, 'epoch', 0, 0)  18.3 us
    all_to_all x1, waiting for transfers between devices, on_device(): lax.all_to_all(total, 'epoch', split_axis=0, concat_axis=1, tiled=True)  14.6 us
    all_to_all x1, starting transfers between devices, on_device(): jax.lax.all_to_all(block_last, 'epoch', 0, 0)  7.33 us
    all_to_all x1, starting transfers between devices, on_device(): lax.all_to_all(total, 'epoch', split_axis=0, concat_axis=1, tiled=True)  3.7 us
    gather x3, local copies, waits for them, and re-layouts, roll_forward(): return lax.dynamic_slice_in_dim(doubled, across, side, 1)  2.97 us
    gather x2, local copies, waits for them, and re-layouts, roll_forward(): rows = lax.dynamic_slice_in_dim(doubled, down, side, 0)  2.71 us
    another operation x1, local copies, waits for them, and re-layouts, on_device(): block_last = jnp.stack(jax.lax.axis_size('epoch') * [model_low], axis=0)  1.65 us
  transfers between devices with their start and end apart: 2, of which 2 were waited for; matrix products, arithmetic and copies ran while one was open for 3% of the time, Pallas kernels for 0%

profile of v1, /device:TPU:0, one launch (start us, length us, event | category | flops | bytes accessed | tf_op | source)
XLA Modules:
  0.0 62.6 jit_solution(17851898040963915639)
XLA Ops:
  0.0 1.1 %convert_bitcast_fusion = bf16[2,6,4096]{2,0,1:T(2,128)(2,1)S(1)} fusion(f32[1,2,6,4096]{3,1,2,0:T(2,128)} %param.10), kind=kLoop, calls=%fused_computation.27 | loop fusion | flops 49152 | bytes 294912 | tf_op jit(solution)/shard_map/convert_element_type | solution.py:60
  1.1 0.0 copy-start.8
  1.1 0.0 copy-start.9
  1.1 0.0 copy-start.7
  1.1 1.7 %stack.2 = bf16[8,1,2,6,4096]{4,2,3,1,0:T(2,128)(2,1)} broadcast(bf16[2,6,4096]{2,0,1:T(2,128)(2,1)S(1)} %convert_bitcast_fusion), dimensions={2,3,4} | broadcast | bytes 884736 | tf_op jit(solution)/shard_map/stack | solution.py:61
  2.8 7.3 %all-to-all-start = ((bf16[8,1,2,6,4096]{4,2,3,1,0:T(2,128)(2,1)}), bf16[8,1,2,6,4096]{4,2,3,1,0:T(2,128)(2,1)S(1)}, u32[]{:S(2)}, u32[]{:S(2)}) async-start(bf16[8,1,2,6,4096]{4,2,3,1,0:T(2,128)(2,1)} %stack.2), calls=%async_computation | async-start | bytes 1572864 | tf_op jit(solution)/shard_map/all_to_all | solution.py:62
  10.1 0.0 copy-done.3
  10.1 0.1 reduce.2
  10.1 0.1 reshape.79
  10.2 0.0 copy-done.4
  10.2 0.1 reduce.3
  10.3 0.1 reshape.80
  10.4 0.0 copy-done.5
  10.4 0.1 reduce
  10.4 0.1 reshape.77
  10.5 0.0 copy-done.6
  10.5 0.1 reduce.1
  10.6 0.1 reshape.78
  10.7 1.0 %reshape.81 = f32[16,64,64]{2,1,0:T(8,128)} reshape(bf16[1,16,4096]{2,1,0:T(8,128)(2,1)S(1)} %copy-done.2) | data formatting | bytes 393216 | tf_op jit(solution)/shard_map/convert_element_type | solution.py:29
  11.7 0.1 fusion.10
  11.8 0.1 fusion.9
  12.0 18.3 %all-to-all-done = bf16[8,1,2,6,4096]{4,2,3,1,0:T(2,128)(2,1)S(1)} async-done(((bf16[8,1,2,6,4096]{4,2,3,1,0:T(2,128)(2,1)}), bf16[8,1,2,6,4096]{4,2,3,1,0:T(2,128)(2,1)S(1)}, u32[]{:S(2)}, u32[]{:S(2)}) %all-to-all-start) | async-done | bytes 786464 | tf_op jit(solution)/shard_map/all_to_all | solution.py:62
  30.3 0.8 %copy.29 = bf16[8,1,2,6,4096]{4,2,0,3,1:T(2,128)(2,1)S(1)} copy(bf16[8,1,2,6,4096]{4,2,3,1,0:T(2,128)(2,1)S(1)} %all-to-all-done) | data formatting | bytes 1572864 | tf_op jit(solution)/shard_map/all_to_all | solution.py:62
  31.0 1.0 %reshape_squeeze_reshape.3 = bf16[16,6,64,64]{3,2,0,1:T(8,128)(2,1)S(1)} reshape(bf16[8,1,2,6,4096]{4,2,0,3,1:T(2,128)(2,1)S(1)} %copy.29) | data formatting | bytes 1572864 | tf_op jit(solution)/shard_map/reshape;squeeze;reshape | solution.py:64
  32.1 0.2 copy.54
  32.3 0.1 pad_maximum_fusion
  32.4 1.4 %gather_fusion = bf16[16,64,64]{2,0,1:T(8,128)(2,1)S(1)} fusion(bf16[16,128,64]{2,0,1:T(8,128)(2,1)S(1)} %pad_maximum_fusion, s32[16]{0:T(128)S(1)} %get-tuple-element.6), kind=kCustom, calls=%fused_computation | custom fusion | bytes 262336 | tf_op jit(solution)/shard_map/vmap()/gather | solution.py:15
  33.8 0.1 pad_maximum_fusion.3
  33.9 0.0 copy-start
  34.0 0.5 copy.31
  34.5 1.4 %gather_fusion.1 = bf16[16,64,64]{1,0,2:T(8,128)(2,1)S(1)} fusion(bf16[16,64,128]{1,0,2:T(8,128)(2,1)S(1)} %copy.31, s32[16]{0:T(128)S(1)} %get-tuple-element.7), kind=kCustom, calls=%fused_computation.1 | custom fusion | bytes 262336 | tf_op jit(solution)/shard_map/vmap()/gather | solution.py:17
  35.9 0.4 fusion.5
  36.3 0.4 fusion.8
  36.8 0.2 pad_maximum_fusion.1
  37.0 0.5 copy.37
  37.5 1.3 %gather_fusion.2 = f32[16,64,64]{2,0,1:T(8,128)S(1)} fusion(f32[16,128,64]{2,0,1:T(8,128)S(1)} %copy.37, s32[16]{0:T(128)S(1)} %get-tuple-element.8), kind=kCustom, calls=%fused_computation.2 | custom fusion | bytes 524480 | tf_op jit(solution)/shard_map/vmap()/gather | solution.py:15
  38.8 0.2 pad_maximum_fusion.2
  39.0 0.6 copy.38
  39.6 1.3 %gather_fusion.3 = f32[16,64,64]{1,0,2:T(8,128)S(1)} fusion(f32[16,64,128]{1,0,2:T(8,128)S(1)} %copy.38, s32[16]{0:T(128)S(1)} %get-tuple-element.5), kind=kCustom, calls=%fused_computation.3 | custom fusion | bytes 524480 | tf_op jit(solution)/shard_map/vmap()/gather | solution.py:17
  41.0 0.3 copy.39
  41.2 0.0 copy-start.10
  41.3 0.3 broadcast_in_dim.8
  41.6 1.0 %dynamic_update_slice.4.clone = f32[16,2,4096]{2,1,0:T(2,128)} pad(f32[16,1,4096]{2,1,0:T(1,128)S(1)} %broadcast_in_dim.8, f32[]{:T(128)} %constant.85.clone.1), padding=0_0x0_1x0_0 | pad | bytes 786436 | tf_op jit(solution)/shard_map/jit(dynamic_update_index_in_dim)/dynamic_update_slice | solution.py:71
  42.6 3.7 %all-to-all-start.1 = ((f32[16,2,4096]{2,1,0:T(2,128)}), f32[16,2,4096]{2,1,0:T(2,128)S(1)}, u32[]{:S(2)}, u32[]{:S(2)}) async-start(f32[16,2,4096]{2,1,0:T(2,128)} %dynamic_update_slice.4.clone), calls=%async_computation.1 | async-start | bytes 1048576 | tf_op jit(solution)/shard_map/all_to_all | solution.py:72
  46.3 14.6 %all-to-all-done.1 = f32[16,2,4096]{2,1,0:T(2,128)S(1)} async-done(((f32[16,2,4096]{2,1,0:T(2,128)}), f32[16,2,4096]{2,1,0:T(2,128)S(1)}, u32[]{:S(2)}, u32[]{:S(2)}) %all-to-all-start.1) | async-done | bytes 524320 | tf_op jit(solution)/shard_map/all_to_all | solution.py:72
  61.0 0.4 all_to_all.20
  61.4 0.4 fusion.3
  61.7 0.8 %copy.42 = f32[1,2,6,4096]{3,1,2,0:T(2,128)} copy(f32[1,2,6,4096]{3,2,1,0:T(8,128)S(1)} %fusion.3) | data formatting | bytes 393216 | tf_op jit(solution)/shard_map/broadcast_in_dim | solution.py:81
  (19 shorter events, 0.1 us)
Async XLA Ops:
  0.0 10.1 %copy-start.3 = (bf16[1,4096]{1,0:T(2,128)(2,1)S(1)}, bf16[1,4096]{1,0:T(2,128)(2,1)}, u32[]{:S(2)}) copy-start(bf16[1,4096]{1,0:T(2,128)(2,1)} %param.18) | copy-start | bytes 24580
  0.0 10.2 %copy-start.4 = (bf16[1,4096]{1,0:T(2,128)(2,1)S(1)}, bf16[1,4096]{1,0:T(2,128)(2,1)}, u32[]{:S(2)}) copy-start(bf16[1,4096]{1,0:T(2,128)(2,1)} %param.19) | copy-start | bytes 24580
  0.0 10.4 %copy-start.5 = (bf16[1,4096]{1,0:T(2,128)(2,1)S(1)}, bf16[1,4096]{1,0:T(2,128)(2,1)}, u32[]{:S(2)}) copy-start(bf16[1,4096]{1,0:T(2,128)(2,1)} %param.16) | copy-start | bytes 24580
  0.0 10.5 %copy-start.6 = (bf16[1,4096]{1,0:T(2,128)(2,1)S(1)}, bf16[1,4096]{1,0:T(2,128)(2,1)}, u32[]{:S(2)}) copy-start(bf16[1,4096]{1,0:T(2,128)(2,1)} %param.17) | copy-start | bytes 24580
  0.0 10.6 %copy-start.2 = (bf16[1,16,4096]{2,1,0:T(8,128)(2,1)S(1)}, bf16[1,16,4096]{2,1,0:T(8,128)(2,1)}, u32[]{:S(2)}) copy-start(bf16[1,16,4096]{2,1,0:T(8,128)(2,1)} %param.11) | copy-start | bytes 393220
  1.1 10.8 %copy-start.8 = (f32[1,16]{1,0:T(1,128)S(1)}, f32[1,16]{1,0:T(1,128)}, u32[]{:S(2)}) copy-start(f32[1,16]{1,0:T(1,128)} %param.12) | copy-start | bytes 196
  1.1 10.8 %copy-start.9 = (s32[1,16]{1,0:T(1,128)S(1)}, s32[1,16]{1,0:T(1,128)}, u32[]{:S(2)}) copy-start(s32[1,16]{1,0:T(1,128)} %param.13) | copy-start | bytes 196
  1.1 10.8 %copy-start.7 = (s32[1,16,2]{1,2,0:T(2,128)S(1)}, s32[1,16,2]{1,2,0:T(2,128)}, u32[]{:S(2)}) copy-start(s32[1,16,2]{1,2,0:T(2,128)} %param.14) | copy-start | bytes 388
  2.8 27.5 %all-to-all-start = ((bf16[8,1,2,6,4096]{4,2,3,1,0:T(2,128)(2,1)}), bf16[8,1,2,6,4096]{4,2,3,1,0:T(2,128)(2,1)S(1)}, u32[]{:S(2)}, u32[]{:S(2)}) async-start(bf16[8,1,2,6,4096]{4,2,3,1,0:T(2,128)(2,1)} %stack.2), calls=%async_computation | async-start | bytes 1572864 | tf_op jit(solution)/shard_map/all_to_all | solution.py:62
  33.9 1.9 %copy-start = (f32[16,64,64]{2,1,0:T(8,128)S(1)}, f32[16,64,64]{2,1,0:T(8,128)}, u32[]{:S(2)}) copy-start(f32[16,64,64]{2,1,0:T(8,128)} %reshape.81) | copy-start | bytes 786436
  41.2 5.1 %copy-start.10 = (s32[1,2]{1,0:T(1,128)S(1)}, s32[1,2]{1,0:T(1,128)}, u32[]{:S(2)}) copy-start(s32[1,2]{1,0:T(1,128)} %param.15) | copy-start | bytes 28
  42.6 18.8 %copy-start.1 = (f32[1,2,6,4096]{3,1,2,0:T(2,128)S(1)}, f32[1,2,6,4096]{3,1,2,0:T(2,128)}, u32[]{:S(2)}) copy-start(f32[1,2,6,4096]{3,1,2,0:T(2,128)} %param.10) | copy-start | bytes 589828
  42.6 18.4 %all-to-all-start.1 = ((f32[16,2,4096]{2,1,0:T(2,128)}), f32[16,2,4096]{2,1,0:T(2,128)S(1)}, u32[]{:S(2)}, u32[]{:S(2)}) async-start(f32[16,2,4096]{2,1,0:T(2,128)} %dynamic_update_slice.4.clone), calls=%async_computation.1 | async-start | bytes 1048576 | tf_op jit(solution)/shard_map/all_to_all | solution.py:72
